TPU v7x, 128 devices: a whole 4x4x4 slice. The times are simulated.
128 devices in a mesh: dp: 16 (over y_hi, x, core), mp: 8 (over z, y_lo).
Axes of the slice: x: 4, y: 4 (y_hi: 2, y_lo: 2; y = y_hi * 2 + y_lo), z: 4, core: 2. Of those that a mesh axis runs over, the one named last changes fastest.
Arguments:
- hidden_states: bfloat16 [65536, 4096], P('dp', 'mp'), may hold values from -1 to 1
- factor_values: bfloat16 [65536, 128], P('dp', 'mp'), may hold values from 0.029907227 to 0.13964844
- class_ids: int32 [65536, 128], P('dp', 'mp'), may hold values from 0 to 128255, as said below
- centers: int32 [3], replicated, may hold values from 0 to 65535
Outputs:
- min_distance: float32 [65536], P(('dp', 'mp'))
- weight_means: float32 [3], replicated
Inputs may be any that keep to these rules, and one draw needn't show every extreme that they name: `centers`: each value is a sample index. `class_ids`: entries k * 16 to (k + 1) * 16 - 1 of a row hold distinct classes of the k-th of 8 equal ranges of the vocabulary.
All inputs are finite; a program needn't handle non-finite values.
Results may differ from a plain program's by a relative error of at most 0.00095.
Values may be sent and summed in bfloat16 or wider, within the bound.
A program may use at most 64 MiB of HBM per device.

v0:
```python
import functools

import jax
import jax.numpy as jnp
from jax import lax
from jax.sharding import Mesh
from jax.sharding import PartitionSpec as P

K_LOC = 16
STEPS = 3
MP = ("mp_0", "mp_1")
DP = ("dp_0", "dp_1", "dp_2")
DP_MP = ("dp_0", "dp_1", "dp_2", "mp_0", "mp_1")


def split_up(shard, dim, length):
    before, after = (shard.shape[:dim], shard.shape[dim + 1 :])
    return jnp.moveaxis(shard.reshape(*before, length, -1, *after), dim, 0)


def summed_on_arrival(shard, axis, dim):
    length = lax.axis_size(axis)
    parts = lax.all_to_all(split_up(shard, dim, length), axis, 0, 0, tiled=True)
    return jnp.sum(parts, axis=0)


def by_axis(shard, axes):
    return functools.reduce(lax.psum, axes, shard)


def match_sum(idents, values, id_row, val_row):
    nblk = idents.shape[1] // K_LOC
    match = idents.reshape(-1, nblk, K_LOC, 1) == id_row.reshape(1, nblk, 1, K_LOC)
    prod = values.astype(jnp.float32).reshape(-1, nblk, K_LOC, 1) * val_row.astype(
        jnp.float32
    ).reshape(1, nblk, 1, K_LOC)
    return jnp.sum(jnp.where(match, prod, jnp.float32(0.0)), axis=(1, 2, 3))


def squares(values):
    return jnp.sum(jnp.square(values.astype(jnp.float32)), axis=1)


def body(hidden_states, factor_values, class_ids, centers):
    partial_sums = []
    min_distance = None
    rows_all = hidden_states.shape[0]
    rows = rows_all // lax.axis_size(MP)
    device_pos = lax.axis_index(DP)
    model_pos = lax.axis_index(MP)
    width_h = hidden_states.shape[1]
    width_a = factor_values.shape[1]
    start_h = model_pos * width_h
    start_a = model_pos * width_a
    full_h = width_h * lax.axis_size(MP)
    full_a = width_a * lax.axis_size(MP)
    owners = centers // rows_all
    offsets = centers - owners * rows_all
    mine = (owners == device_pos).astype(jnp.float32)[:, None]
    pick_h = hidden_states[offsets].astype(jnp.float32) * mine
    pick_v = factor_values[offsets].astype(jnp.float32) * mine
    pick_i = class_ids[offsets].astype(jnp.float32) * mine
    count = centers.shape[0]
    table_h = lax.dynamic_update_slice(
        jnp.zeros((count, full_h), jnp.float32), pick_h, (0, start_h)
    )
    table_v = lax.dynamic_update_slice(
        jnp.zeros((count, full_a), jnp.float32), pick_v, (0, start_a)
    )
    table_i = lax.dynamic_update_slice(
        jnp.zeros((count, full_a), jnp.float32), pick_i, (0, start_a)
    )
    table_h, table_v, table_i = lax.psum((table_h, table_v, table_i), DP_MP)
    center_hn = jnp.sum(table_h * table_h, axis=1)
    center_an = jnp.sum(table_v * table_v, axis=1)
    local_h = lax.dynamic_slice_in_dim(table_h, start_h, width_h, 1).astype(jnp.bfloat16)
    local_v = lax.dynamic_slice_in_dim(table_v, start_a, width_a, 1).astype(jnp.bfloat16)
    local_i = lax.dynamic_slice_in_dim(table_i, start_a, width_a, 1).astype(jnp.int32)
    prods_h = jnp.dot(hidden_states, local_h.T, preferred_element_type=jnp.float32)
    prods_a = [
        match_sum(class_ids, factor_values, local_i[step], local_v[step]) for step in range(STEPS)
    ]
    pieces = [squares(hidden_states), squares(factor_values)]
    pieces = pieces + [prods_h[:, step] for step in range(STEPS)] + prods_a
    summed = summed_on_arrival(jnp.stack(pieces), MP, 1)
    sq_h = summed[0]
    sq_a = summed[1]
    pool_total = rows * lax.axis_size(DP) * lax.axis_size(MP)
    for step in range(STEPS):
        inner_h = summed[2 + step]
        inner_a = summed[2 + STEPS + step]
        norm_hc = center_hn[step]
        norm_ac = center_an[step]
        dist = jnp.maximum(
            sq_h * sq_a + norm_hc * norm_ac - 2.0 * inner_h * inner_a, jnp.float32(0.0)
        )
        min_distance = dist if step == 0 else jnp.minimum(min_distance, dist)
        partial_sums.append(jnp.sum(min_distance))
    weight_means = by_axis(jnp.stack(partial_sums), DP_MP) / pool_total
    return (min_distance, weight_means)


def solution(mesh):
    finer = Mesh(mesh.devices.reshape(2, 4, 2, 4, 2), ("dp_0", "dp_1", "dp_2", "mp_0", "mp_1"))
    return jax.shard_map(
        body,
        mesh=finer,
        in_specs=(P(DP, MP), P(DP, MP), P(DP, MP), P()),
        out_specs=(P(DP_MP), P()),
        check_vma=False,
    )
```

profile of v0, /device:TPU:1, one launch (start us, length us, event | category | flops | bytes accessed | tf_op | source)
XLA Modules:
  0.0 135.3 jit_solution(7775207025141159430)
XLA Ops:
  0.6 1.4 %copy.18 = bf16[4096,16]{1,0:T(8,128)(2,1)S(1)} copy(bf16[4096,16]{0,1:T(8,128)(2,1)} %param.5) | data formatting | bytes 262144 | tf_op args[1]
  2.0 1.6 %convert_element_type.61 = f32[4096,16]{0,1:T(8,128)} convert(bf16[4096,16]{0,1:T(8,128)(2,1)} %param.5) | non-fusion elementwise | flops 65536 | bytes 393216 | tf_op jit(solution)/shard_map/convert_element_type | solution.py:41
  3.6 1.0 multiply_reduce_fusion.1
  4.6 0.7 compare_convert_fusion
  5.3 0.7 compare_select_fusion
  5.9 1.5 %copy.17 = s32[4096,16]{1,0:T(8,128)S(1)} copy(s32[4096,16]{0,1:T(8,128)} %param.6) | data formatting | bytes 524288 | tf_op args[2]
  7.5 3.1 %multiply_reduce_fusion = f32[4096]{0:T(1024)S(1)} fusion(bf16[4096,512]{1,0:T(8,128)(2,1)} %param.4), kind=kLoop, calls=%fused_computation.3 | loop fusion | flops 6287360 | bytes 4210688 | tf_op jit(solution)/shard_map/reduce_sum | solution.py:41
  10.6 3.3 %gather_fusion = bf16[3,512]{1,0:T(4,128)(2,1)S(1)} fusion(bf16[4096,512]{1,0:T(8,128)(2,1)} %param.4, s32[1024]{0:T(1024)S(1)} %pad_clamp_fusion), kind=kCustom, calls=%fused_computation | custom fusion | bytes 6156 | tf_op jit(solution)/shard_map/gather | solution.py:60
  13.9 0.6 gather_fusion.1
  14.5 0.6 gather_fusion.2
  15.1 0.1 dynamic_update_slice.10
  15.3 0.1 dynamic_update_slice.11
  15.4 0.1 multiply_dynamic-update-slice_fusion
  15.5 69.3 %all-reduce = (f32[3,4096]{1,0:T(4,128)S(1)}, f32[3,128]{1,0:T(4,128)S(1)}, f32[3,128]{1,0:T(4,128)S(1)}) all-reduce(f32[3,4096]{1,0:T(4,128)S(1)} %multiply_dynamic-update-slice_fusion, f32[3,128]{1,0:T(4,128)S(1)} %dynamic_update_slice.11, ...), channel_id=1, replica_groups=mesh['dp_0'=2,'dp_1'=4,'dp_2'=2,'mp_0'=4,'mp_1'=2] {'dp_0','dp_1','dp_2'..., use_global_device_ids=true, to_apply=%region_2.3 | all-reduce | flops 13056 | bytes 104448 | tf_op jit(solution)/shard_map/psum | solution.py:73
  85.0 3.4 %convolution_bitcast_fusion = f32[4096,3]{0,1:T(4,128)S(1)} fusion(bf16[4096,512]{1,0:T(8,128)(2,1)} %param.4, f32[3,4096]{1,0:T(4,128)S(1)} %get-tuple-element.5, s32[]{:T(128)S(6)} %select_n.56), kind=kOutput, calls=%fused_computation.4 | convolution fusion | flops 12582912 | bytes 4247556 | tf_op jit(solution)/shard_map/dot_general | solution.py:79
  88.4 2.0 %select_reduce_fusion = (f32[4096]{0:T(1024)S(1)}, f32[4096]{0:T(1024)S(1)}, f32[4096]{0:T(1024)S(1)}) fusion(f32[16]{0:T(128)S(1)} %get-tuple-element.24, f32[4096,16]{0,1:T(8,128)S(1)} %copy-done.1, s32[4096,16]{0,1:T(8,128)S(1)} %copy-done, s32[16]{0:T(128)S(1)} %get-tuple-element.21, f32[16]{0:T(128)S(1)} %get-tuple-element.25, ...), kind=kLoop, calls=%fused_computation.5 | loop fusion | flops 12570624 | bytes 573824 | tf_op jit(solution)/shard_map/reduce_sum | solution.py:37
  90.4 0.8 stack.44
  91.2 3.4 %all-to-all-start = ((f32[8,8,512]{2,1,0:T(8,128)}), f32[8,8,512]{2,1,0:T(8,128)S(1)}, u32[]{:S(2)}, u32[]{:S(2)}) async-start(f32[8,8,512]{2,1,0:T(8,128)} %bitcast.15), calls=%async_computation | async-start | bytes 262144 | tf_op jit(solution)/shard_map/all_to_all | solution.py:23
  94.6 0.1 multiply_reduce_fusion.2
  94.8 0.1 multiply_reduce_fusion.3
  94.9 0.7 fusion.10
  99.4 0.8 all-to-all-done
  100.2 0.7 fusion.5
  100.9 0.6 fusion.7
  101.5 1.2 fusion.8
  102.7 2.0 %pad_maximum_fusion = f32[3]{0:T(128)S(1)} fusion(f32[1]{0:T(128)} %bitcast.22, f32[1]{0:T(128)} %bitcast.21, f32[1]{0:T(128)} %bitcast.20), kind=kLoop, calls=%fused_computation.38 | loop fusion | flops 6 | bytes 24 | tf_op jit(solution)/shard_map/stack | solution.py:99
  104.6 5.3 %psum.59 = f32[3]{0:T(128)S(1)} all-reduce(f32[3]{0:T(128)S(1)} %pad_maximum_fusion), channel_id=1, replica_groups=mesh['dp_0'=2,'dp_1'=4,'dp_2'=2,'mp_0'=4,'mp_1'=2] {'dp_0'}, use_global_device_ids=true, to_apply=%region_14.15 | all-reduce | flops 3 | bytes 24 | tf_op jit(solution)/shard_map/psum | solution.py:28
  109.9 6.5 %psum.60 = f32[3]{0:T(128)S(1)} all-reduce(f32[3]{0:T(128)S(1)} %psum.59), channel_id=1, replica_groups=mesh['dp_0'=2,'dp_1'=4,'dp_2'=2,'mp_0'=4,'mp_1'=2] {'dp_1'}, use_global_device_ids=true, to_apply=%region_15.16 | all-reduce | flops 3 | bytes 24 | tf_op jit(solution)/shard_map/psum | solution.py:28
  116.4 7.6 %psum.61 = f32[3]{0:T(128)S(1)} all-reduce(f32[3]{0:T(128)S(1)} %psum.60), channel_id=1, replica_groups=mesh['dp_0'=2,'dp_1'=4,'dp_2'=2,'mp_0'=4,'mp_1'=2] {'dp_2'}, use_global_device_ids=true, to_apply=%region_16.17 | all-reduce | flops 3 | bytes 24 | tf_op jit(solution)/shard_map/psum | solution.py:28
  124.0 7.0 %psum.62 = f32[3]{0:T(128)S(1)} all-reduce(f32[3]{0:T(128)S(1)} %psum.61), channel_id=1, replica_groups=mesh['dp_0'=2,'dp_1'=4,'dp_2'=2,'mp_0'=4,'mp_1'=2] {'mp_0'}, use_global_device_ids=true, to_apply=%region_17.18 | all-reduce | flops 3 | bytes 24 | tf_op jit(solution)/shard_map/psum | solution.py:28
  131.0 3.8 %psum.63 = f32[3]{0:T(128)S(1)} all-reduce(f32[3]{0:T(128)S(1)} %psum.62), channel_id=1, replica_groups=mesh['dp_0'=2,'dp_1'=4,'dp_2'=2,'mp_0'=4,'mp_1'=2] {'mp_1'}, use_global_device_ids=true, to_apply=%region_18.19 | all-reduce | flops 3 | bytes 24 | tf_op jit(solution)/shard_map/psum | solution.py:28
  134.8 0.5 broadcast_multiply_fusion
  (15 shorter events, 0.3 us)
Async XLA Ops:
  7.5 80.9 %copy-start = (s32[4096,16]{0,1:T(8,128)S(1)}, s32[4096,16]{0,1:T(8,128)}, u32[]{:S(2)}) copy-start(s32[4096,16]{0,1:T(8,128)} %param.6) | copy-start | bytes 786436
  14.5 73.9 %copy-start.1 = (f32[4096,16]{0,1:T(8,128)S(1)}, f32[4096,16]{0,1:T(8,128)}, u32[]{:S(2)}) copy-start(f32[4096,16]{0,1:T(8,128)} %convert_element_type.61) | copy-start | bytes 786436
  91.2 8.9 %all-to-all-start = ((f32[8,8,512]{2,1,0:T(8,128)}), f32[8,8,512]{2,1,0:T(8,128)S(1)}, u32[]{:S(2)}, u32[]{:S(2)}) async-start(f32[8,8,512]{2,1,0:T(8,128)} %bitcast.15), calls=%async_computation | async-start | bytes 262144 | tf_op jit(solution)/shard_map/all_to_all | solution.py:23
where the time goes:
time: 138 us; the launch traced here: 135 us
  blocking collectives  99.5 us (72%)
  other arithmetic  14.5 us (11%)
  local copies, waits for them, and re-layouts  9.23 us (7%)
  between operations  4.63 us (3%)
  starting transfers between devices  3.37 us (2%)
  matrix products  3.36 us (2%)
    psum x1, blocking collectives, body(): table_h, table_v, table_i = lax.psum((table_h, table_v, table_i), DP_MP)  69.3 us
    psum x5, blocking collectives, by_axis(): return functools.reduce(lax.psum, axes, shard)  30.1 us
    reduce_sum x2, other arithmetic, squares(): return jnp.sum(jnp.square(values.astype(jnp.float32)), axis=1)  4.08 us
    all_to_all x1, starting transfers between devices, summed_on_arrival(): parts = lax.all_to_all(split_up(shard, dim, length), axis, 0, 0, tiled=True)  3.37 us
    dot_general x1, matrix products, body(): jnp.dot(hidden_states, local_h.T, preferred_element_type=jnp.float32)  3.36 us
    gather x1, local copies, waits for them, and re-layouts, body(): pick_h = hidden_states[offsets].astype(jnp.float32) * mine  3.29 us
    unnamed x6, local copies, waits for them, and re-layouts  2.94 us
  transfers between devices with their start and end apart: 1, of which 1 were waited for; matrix products, arithmetic and copies ran while one was open for 1% of the time, Pallas kernels for 0%

commit v1 on v0

v1 whole, which is shorter than its diff:
```python
import functools

import jax
import jax.numpy as jnp
from jax import lax
from jax.experimental import pallas as pl
from jax.experimental.pallas import tpu as pltpu
from jax.sharding import PartitionSpec as P

STEPS = 3
VOCAB = 128256
MESH = pl.DeviceIdType.MESH
F32 = jnp.float32
BF16 = jnp.bfloat16
NT = (((1,), (1,)), ((), ()))


def iota(shape, dim):
    return lax.broadcasted_iota(jnp.int32, shape, dim)


def kernel(
    n_dp, n_mp, pool,
    h_hbm, v_hbm, i_hbm, cen, min_ref, mean_ref,
    h, v, ids, abuf, nbuf, bsend, bbuf, m1, m2,
    load_sem, a_send, a_recv, n_send, n_recv, b_send, b_recv, s1, r1, s2, r2,
):
    dp, mp = lax.axis_index("dp"), lax.axis_index("mp")
    groups, _, width = h.shape
    rows_all = groups * 16
    k_loc = v.shape[0]
    rows = rows_all // n_mp
    q_n = width // 128

    loads = [
        pltpu.make_async_copy(h_hbm, h, load_sem.at[0]),
        pltpu.make_async_copy(v_hbm, v, load_sem.at[1]),
        pltpu.make_async_copy(i_hbm, ids, load_sem.at[2]),
    ]
    for copy in loads:
        copy.start()

    barrier = pltpu.get_barrier_semaphore()
    for r in range(1, n_dp):
        pl.semaphore_signal(
            barrier, inc=1, device_id={"dp": lax.rem(dp + r, n_dp), "mp": mp}, device_id_type=MESH
        )
    for r in range(1, n_mp):
        pl.semaphore_signal(
            barrier, inc=1, device_id={"dp": dp, "mp": lax.rem(mp + r, n_mp)}, device_id_type=MESH
        )

    def send(src, dst, s_sem, r_sem, d, m):
        copy = pltpu.make_async_remote_copy(
            src_ref=src, dst_ref=dst, send_sem=s_sem, recv_sem=r_sem,
            device_id={"dp": d, "mp": m}, device_id_type=MESH,
        )
        copy.start()

    def settle(ref, s_sem, r_sem):
        return pltpu.make_async_remote_copy(
            src_ref=ref, dst_ref=ref, send_sem=s_sem, recv_sem=r_sem,
            device_id={"dp": dp, "mp": mp}, device_id_type=MESH,
        )

    for copy in loads:
        copy.wait()

    row16, lane16 = iota((16, 128), 0), iota((16, 128), 1)
    msg = jnp.zeros((16, 128), F32)
    wide = iota((16, rows_all), 1)
    base = mp * (VOCAB // n_mp)
    for j in range(STEPS):
        c = cen[j]
        loc = lax.rem(c, rows_all)
        mine = c - dp * rows_all
        start_r = loc - lax.rem(loc, 16)
        blk = h[lax.div(loc, 16)].astype(F32)
        pick_r = iota((16, width), 0) == mine - start_r
        row = jnp.sum(jnp.where(pick_r, blk, 0.0), axis=0, keepdims=True)
        for q in range(q_n):
            piece = row[:, q * 128 : (q + 1) * 128]
            msg = jnp.where(row16 == j * q_n + q, piece, msg)
        pick_l = wide == mine
        rel = jnp.sum(jnp.where(pick_l, ids[...] - base, 0), axis=1, keepdims=True)
        val = jnp.sum(jnp.where(pick_l, v[...].astype(F32), 0.0), axis=1, keepdims=True)
        hi = lax.shift_right_logical(rel, 7)
        lo = jnp.bitwise_and(rel, 127)
        parts = [val, hi.astype(F32), lo.astype(F32)]
        spread = jnp.zeros((16, 128), F32)
        for p, col in enumerate(parts):
            spread = jnp.where(lane16 == row16 + p * k_loc, col, spread)
        line = jnp.sum(spread, axis=0, keepdims=True)
        msg = jnp.where(row16 == STEPS * q_n + j, line, msg)
    abuf[dp] = msg.astype(BF16)

    pl.semaphore_wait(barrier, n_dp - 1 + n_mp - 1)
    for r in range(1, n_dp):
        send(abuf.at[dp], abuf.at[dp], a_send, a_recv, lax.rem(dp + r, n_dp), mp)

    ones = jnp.ones((16, 256), BF16)
    for r in range(n_mp):
        hc = h[pl.ds(r * (rows // 16), rows // 16)].reshape(rows, width).astype(F32)
        sq = hc * hc
        part = sq[:, 0:128]
        for q in range(1, q_n):
            part = part + sq[:, q * 128 : (q + 1) * 128]
        hi = part.astype(BF16)
        lo = (part - hi.astype(F32)).astype(BF16)
        both = jnp.concatenate([hi, lo], axis=1)
        sums = lax.dot_general(ones, both, NT, preferred_element_type=F32)
        bsend[r, 0:1, :] = sums[0:1, :]
        vc = v[:, pl.ds(r * rows, rows)].astype(F32)
        bsend[r, 1:2, :] = jnp.sum(vc * vc, axis=0, keepdims=True)

    settle(abuf.at[pl.ds(0, n_dp - 1)], a_send, a_recv).wait_recv()
    tot = jnp.zeros((16, 128), F32)
    for d in range(n_dp):
        tot = tot + abuf[d].astype(F32)

    keep = jnp.logical_or(row16 < STEPS * q_n, lane16 < k_loc)
    sums = jnp.sum(jnp.where(keep, tot * tot, 0.0), axis=1, keepdims=True)
    first = jnp.logical_and(row16 < STEPS * q_n, lane16 == lax.shift_right_logical(row16, 2))
    second = jnp.logical_and(row16 >= STEPS * q_n, lane16 == row16 - STEPS * q_n + 8)
    line = jnp.sum(jnp.where(jnp.logical_or(first, second), sums, 0.0), axis=0, keepdims=True)
    nbuf[mp] = line
    for r in range(1, n_mp):
        send(nbuf.at[mp], nbuf.at[mp], n_send, n_recv, dp, lax.rem(mp + r, n_mp))

    row8 = iota((16, 128), 0)
    cparts = []
    for q in range(q_n):
        part = jnp.zeros((16, 128), F32)
        for j in range(STEPS):
            part = jnp.where(row8 == j, tot[j * q_n + q : j * q_n + q + 1, :], part)
        cparts.append(part)
    cmat = jnp.concatenate(cparts, axis=1).astype(BF16)

    cvals, cids = [], []
    for j in range(STEPS):
        line = tot[STEPS * q_n + j : STEPS * q_n + j + 1, :]
        for k in range(k_loc):
            cvals.append(line[:, k : k + 1])
            hi = line[:, k_loc + k : k_loc + k + 1]
            lo = line[:, 2 * k_loc + k : 2 * k_loc + k + 1]
            cids.append((hi * 128.0 + lo).astype(jnp.int32) + base)

    for r in list(range(1, n_mp)) + [0]:
        to = lax.rem(mp + r, n_mp)
        start = pl.multiple_of(to * rows, rows)
        hc = h[pl.ds(to * (rows // 16), rows // 16)].reshape(rows, width)
        inner = lax.dot_general(cmat, hc, NT, preferred_element_type=F32)
        bsend[to, 2 : 2 + STEPS, :] = inner[0:STEPS, :]
        vc = v[:, pl.ds(start, rows)].astype(F32)
        ic = ids[:, pl.ds(start, rows)]
        for j in range(STEPS):
            w = jnp.zeros((k_loc, rows), F32)
            for k in range(k_loc):
                w = jnp.where(ic == cids[j * k_loc + k], cvals[j * k_loc + k], w)
            bsend[to, 2 + STEPS + j : 3 + STEPS + j, :] = jnp.sum(vc * w, axis=0, keepdims=True)
        if r:
            send(bsend.at[to], bbuf.at[mp], b_send, b_recv, dp, to)
    bbuf[mp] = bsend[mp]

    settle(nbuf.at[pl.ds(0, n_mp - 1)], n_send, n_recv).wait_recv()
    settle(bbuf.at[pl.ds(0, n_mp - 1)], b_send, b_recv).wait_recv()
    full, norms = bbuf[0], nbuf[0]
    for m in range(1, n_mp):
        full = full + bbuf[m]
        norms = norms + nbuf[m]

    both = full[0:1, :] * full[1:2, :]
    lane = iota((1, 128), 1)
    line = jnp.zeros((1, 128), F32)
    least = None
    for j in range(STEPS):
        own = norms[:, j : j + 1] * norms[:, 8 + j : 9 + j]
        cross = 2.0 * full[2 + j : 3 + j, :] * full[2 + STEPS + j : 3 + STEPS + j, :]
        dist = jnp.maximum(both + own - cross, 0.0)
        least = dist if j == 0 else jnp.minimum(least, dist)
        line = jnp.where(lane == j, jnp.sum(least, axis=1, keepdims=True), line)
    min_ref[...] = least

    m1[mp] = line
    for r in range(1, n_mp):
        send(m1.at[mp], m1.at[mp], s1, r1, dp, lax.rem(mp + r, n_mp))
    settle(m1.at[pl.ds(0, n_mp - 1)], s1, r1).wait_recv()
    line = m1[0]
    for m in range(1, n_mp):
        line = line + m1[m]
    m2[dp] = line
    for r in range(1, n_dp):
        send(m2.at[dp], m2.at[dp], s2, r2, lax.rem(dp + r, n_dp), mp)
    settle(m2.at[pl.ds(0, n_dp - 1)], s2, r2).wait_recv()
    line = m2[0]
    for d in range(1, n_dp):
        line = line + m2[d]
    mean_ref[...] = line * (1.0 / pool)

    settle(abuf.at[pl.ds(0, n_dp - 1)], a_send, a_recv).wait_send()
    settle(nbuf.at[pl.ds(0, n_mp - 1)], n_send, n_recv).wait_send()
    settle(bbuf.at[pl.ds(0, n_mp - 1)], b_send, b_recv).wait_send()
    settle(m1.at[pl.ds(0, n_mp - 1)], s1, r1).wait_send()
    settle(m2.at[pl.ds(0, n_dp - 1)], s2, r2).wait_send()


def body(n_dp, n_mp, hidden_states, factor_values, class_ids, centers):
    rows_all, width = hidden_states.shape
    k_loc = factor_values.shape[1]
    rows = rows_all // n_mp
    dma = pltpu.SemaphoreType.DMA
    least, means = pl.pallas_call(
        functools.partial(kernel, n_dp, n_mp, rows_all * n_dp),
        out_shape=(
            jax.ShapeDtypeStruct((1, rows), F32),
            jax.ShapeDtypeStruct((1, 128), F32),
        ),
        in_specs=[pl.BlockSpec(memory_space=pl.ANY)] * 3
        + [pl.BlockSpec(memory_space=pltpu.SMEM)],
        out_specs=(pl.BlockSpec(memory_space=pltpu.VMEM),) * 2,
        scratch_shapes=[
            pltpu.VMEM((rows_all // 16, 16, width), BF16),
            pltpu.VMEM((k_loc, rows_all), BF16),
            pltpu.VMEM((k_loc, rows_all), jnp.int32),
            pltpu.VMEM((n_dp, 16, 128), BF16),
            pltpu.VMEM((n_mp, 1, 128), F32),
            pltpu.VMEM((n_mp, 8, rows), F32),
            pltpu.VMEM((n_mp, 8, rows), F32),
            pltpu.VMEM((n_mp, 1, 128), F32),
            pltpu.VMEM((n_dp, 1, 128), F32),
            dma((3,)),
        ]
        + [dma(())] * 10,
        compiler_params=pltpu.CompilerParams(collective_id=0, has_side_effects=True),
        name="badge",
    )(hidden_states.reshape(rows_all // 16, 16, width), factor_values.T, class_ids.T, centers)
    return least.reshape(rows), means[0, :STEPS]


def solution(mesh):
    return jax.shard_map(
        functools.partial(body, mesh.shape["dp"], mesh.shape["mp"]),
        mesh=mesh,
        in_specs=(P("dp", "mp"), P("dp", "mp"), P("dp", "mp"), P()),
        out_specs=(P(("dp", "mp")), P()),
        check_vma=False,
    )
```

time: 138 us -> 32.4 us (0.23); the launches traced: 135 us -> 32.3 us
  blocking collectives: 99.5 us -> 0 us
  Pallas kernels: 0 us -> 29.3 us
  other arithmetic: 14.5 us -> 0 us
  local copies, waits for them, and re-layouts: 9.23 us -> 2.39 us
  between operations: 4.63 us -> 0.64 us
  starting transfers between devices: 3.37 us -> 0 us
  matrix products: 3.36 us -> 0 us
    psum x6 -> x0, blocking collectives: 99.5 us -> none  [the longest x1 69.3 us: body(): table_h, table_v, table_i = lax.psum((table_h, table_v, table_i), DP_MP)]
    pallas_call x0 -> x1, Pallas kernels: none -> 29.3 us  [body(): pl.pallas_call(functools.partial(kernel, n_dp, n_mp, rows_all * n_dp), ou...]
    reduce_sum x9 -> x0, other arithmetic: 8.8 us -> none  [the longest x2 4.08 us: squares(): return jnp.sum(jnp.square(values.astype(jnp.float32)), axis=1)]
    gather x3 -> x0, local copies, waits for them, and re-layouts: 4.41 us -> none  [the longest x1 3.29 us: body(): pick_h = hidden_states[offsets].astype(jnp.float32) * mine]
    all_to_all x1 -> x0, starting transfers between devices: 3.37 us -> none  [summed_on_arrival(): parts = lax.all_to_all(split_up(shard, dim, length), axis, 0, 0, tiled=True)]
    dot_general x1 -> x0, matrix products: 3.36 us -> none  [body(): jnp.dot(hidden_states, local_h.T, preferred_element_type=jnp.float32)]
    convert_element_type x4 -> x0, other arithmetic: 2.37 us -> none  [the longest x1 1.62 us: squares(): return jnp.sum(jnp.square(values.astype(jnp.float32)), axis=1)]
    another operation x1 -> x0, other arithmetic: 1.97 us -> none  [body(): weight_means = by_axis(jnp.stack(partial_sums), DP_MP) / pool_total]
  transfers between devices with their start and end apart: 1 -> 0, of which waited for: 1 -> 0; matrix products, arithmetic and copies ran while one was open for 1% -> 0% of each run, Pallas kernels for 0% -> 0%
where the time goes in v1:
time: 32.4 us; the launch traced here: 32.3 us
  Pallas kernels  29.3 us (90%)
  local copies, waits for them, and re-layouts  2.39 us (7%)
  between operations  0.64 us (2%)
    pallas_call x1, Pallas kernels, body(): pl.pallas_call(functools.partial(kernel, n_dp, n_mp, rows_all * n_dp), ou...  29.3 us
    unnamed x1, local copies, waits for them, and re-layouts  1.25 us
    squeeze x1, local copies, waits for them, and re-layouts, body(): return (least.reshape(rows), means[0, :STEPS])  1.14 us

profile of v1, /device:TPU:1, one launch (start us, length us, event | category | flops | bytes accessed | tf_op | source)
XLA Modules:
  0.0 32.3 jit_solution(18348997802847946571)
XLA Ops:
  0.6 29.3 %badge.1 = (f32[1,512]{1,0:T(1,128)}, f32[1,128]{1,0:T(1,128)}) custom-call(bf16[256,16,512]{2,1,0:T(8,128)(2,1)} %bitcast.6, bf16[16,4096]{1,0:T(8,128)(2,1)} %bitcast.8, s32[16,4096]{1,0:T(8,128)} %bitcast.7, s32[3]{0:T(128)} %cen.1), custom_call_target="tpu_custom_call" | custom-call | tf_op jit(solution)/shard_map/badge/pallas_call | solution.py:212
  29.9 1.1 %slice_bitcast_fusion = f32[3]{0:T(128)} fusion(f32[1,128]{1,0:T(1,128)} %get-tuple-element.5), kind=kLoop, calls=%fused_computation | loop fusion | bytes 24 | tf_op jit(solution)/shard_map/squeeze | solution.py:237
  31.0 1.2 %copy.7 = f32[512]{0:T(512)} copy(f32[512]{0:T(512)} %bitcast.9) | data formatting | bytes 4096

commit v2 on v1

--- a/solution.py
+++ b/solution.py
@@ -1,4 +1,5 @@
 import functools
+import itertools
 
 import jax
 import jax.numpy as jnp
@@ -21,9 +22,9 @@
 
 def kernel(
     n_dp, n_mp, pool,
-    h_hbm, v_hbm, i_hbm, cen, min_ref, mean_ref,
-    h, v, ids, abuf, nbuf, bsend, bbuf, m1, m2,
-    load_sem, a_send, a_recv, n_send, n_recv, b_send, b_recv, s1, r1, s2, r2,
+    h_hbm, v_hbm, i_hbm, c_hbm, min_ref, mean_ref,
+    h, v, ids, cen, abuf, nbuf, bsend, bbuf, mbuf,
+    load_sem, a_send, a_recv, n_send, n_recv, b_send, b_recv, m_send, m_recv,
 ):
     dp, mp = lax.axis_index("dp"), lax.axis_index("mp")
     groups, _, width = h.shape
@@ -36,19 +37,31 @@
         pltpu.make_async_copy(h_hbm, h, load_sem.at[0]),
         pltpu.make_async_copy(v_hbm, v, load_sem.at[1]),
         pltpu.make_async_copy(i_hbm, ids, load_sem.at[2]),
+        pltpu.make_async_copy(c_hbm, cen, load_sem.at[3]),
     ]
     for copy in loads:
         copy.start()
 
+    core, x, y_hi = lax.rem(dp, 2), lax.rem(lax.div(dp, 2), 4), lax.div(dp, 8)
+    y_lo, z = lax.rem(mp, 2), lax.div(mp, 2)
+    dp_at = [
+        (lax.rem(y_hi + a, 2) * 4 + lax.rem(x + b, 4)) * 2 + lax.rem(core + c, 2)
+        for a, b, c in sorted(
+            itertools.product(range(2), range(4), range(2)),
+            key=lambda t: -(4 * t[0] + 2 * min(t[1], 4 - t[1]) + t[2]),
+        )[:-1]
+    ]
+    mp_at = [
+        lax.rem(z + a, 4) * 2 + lax.rem(y_lo + b, 2)
+        for a, b in sorted(
+            itertools.product(range(4), range(2)), key=lambda t: -(min(t[0], 4 - t[0]) + t[1])
+        )[:-1]
+    ]
     barrier = pltpu.get_barrier_semaphore()
-    for r in range(1, n_dp):
-        pl.semaphore_signal(
-            barrier, inc=1, device_id={"dp": lax.rem(dp + r, n_dp), "mp": mp}, device_id_type=MESH
-        )
-    for r in range(1, n_mp):
-        pl.semaphore_signal(
-            barrier, inc=1, device_id={"dp": dp, "mp": lax.rem(mp + r, n_mp)}, device_id_type=MESH
-        )
+    for d in dp_at:
+        pl.semaphore_signal(barrier, inc=1, device_id={"dp": d, "mp": mp}, device_id_type=MESH)
+    for m in mp_at:
+        pl.semaphore_signal(barrier, inc=1, device_id={"dp": dp, "mp": m}, device_id_type=MESH)
 
     def send(src, dst, s_sem, r_sem, d, m):
         copy = pltpu.make_async_remote_copy(
@@ -95,8 +108,8 @@
     abuf[dp] = msg.astype(BF16)
 
     pl.semaphore_wait(barrier, n_dp - 1 + n_mp - 1)
-    for r in range(1, n_dp):
-        send(abuf.at[dp], abuf.at[dp], a_send, a_recv, lax.rem(dp + r, n_dp), mp)
+    for d in dp_at:
+        send(abuf.at[dp], abuf.at[dp], a_send, a_recv, d, mp)
 
     ones = jnp.ones((16, 256), BF16)
     for r in range(n_mp):
@@ -124,8 +137,8 @@
     second = jnp.logical_and(row16 >= STEPS * q_n, lane16 == row16 - STEPS * q_n + 8)
     line = jnp.sum(jnp.where(jnp.logical_or(first, second), sums, 0.0), axis=0, keepdims=True)
     nbuf[mp] = line
-    for r in range(1, n_mp):
-        send(nbuf.at[mp], nbuf.at[mp], n_send, n_recv, dp, lax.rem(mp + r, n_mp))
+    for m in mp_at:
+        send(nbuf.at[mp], nbuf.at[mp], n_send, n_recv, dp, m)
 
     row8 = iota((16, 128), 0)
     cparts = []
@@ -145,20 +158,29 @@
             lo = line[:, 2 * k_loc + k : 2 * k_loc + k + 1]
             cids.append((hi * 128.0 + lo).astype(jnp.int32) + base)
 
-    for r in list(range(1, n_mp)) + [0]:
-        to = lax.rem(mp + r, n_mp)
+    def inner(to):
+        hc = h[pl.ds(to * (rows // 16), rows // 16)].reshape(rows, width)
+        return lax.dot_general(cmat, hc, NT, preferred_element_type=F32)
+
+    order = mp_at + [mp]
+    ahead = inner(order[0])
+    for n, to in enumerate(order):
+        now = ahead
+        if n + 1 < n_mp:
+            ahead = inner(order[n + 1])
         start = pl.multiple_of(to * rows, rows)
-        hc = h[pl.ds(to * (rows // 16), rows // 16)].reshape(rows, width)
-        inner = lax.dot_general(cmat, hc, NT, preferred_element_type=F32)
-        bsend[to, 2 : 2 + STEPS, :] = inner[0:STEPS, :]
         vc = v[:, pl.ds(start, rows)].astype(F32)
         ic = ids[:, pl.ds(start, rows)]
+        found = []
         for j in range(STEPS):
             w = jnp.zeros((k_loc, rows), F32)
             for k in range(k_loc):
                 w = jnp.where(ic == cids[j * k_loc + k], cvals[j * k_loc + k], w)
-            bsend[to, 2 + STEPS + j : 3 + STEPS + j, :] = jnp.sum(vc * w, axis=0, keepdims=True)
-        if r:
+            found.append(jnp.sum(vc * w, axis=0, keepdims=True))
+        bsend[to, 2 : 2 + STEPS, :] = now[0:STEPS, :]
+        for j in range(STEPS):
+            bsend[to, 2 + STEPS + j : 3 + STEPS + j, :] = found[j]
+        if n + 1 < n_mp:
             send(bsend.at[to], bbuf.at[mp], b_send, b_recv, dp, to)
     bbuf[mp] = bsend[mp]
 
@@ -181,27 +203,33 @@
         line = jnp.where(lane == j, jnp.sum(least, axis=1, keepdims=True), line)
     min_ref[...] = least
 
-    m1[mp] = line
-    for r in range(1, n_mp):
-        send(m1.at[mp], m1.at[mp], s1, r1, dp, lax.rem(mp + r, n_mp))
-    settle(m1.at[pl.ds(0, n_mp - 1)], s1, r1).wait_recv()
-    line = m1[0]
-    for m in range(1, n_mp):
-        line = line + m1[m]
-    m2[dp] = line
-    for r in range(1, n_dp):
-        send(m2.at[dp], m2.at[dp], s2, r2, lax.rem(dp + r, n_dp), mp)
-    settle(m2.at[pl.ds(0, n_dp - 1)], s2, r2).wait_recv()
-    line = m2[0]
-    for d in range(1, n_dp):
-        line = line + m2[d]
+    me = dp * n_mp + mp
+    mbuf[me] = line
+    moves = sorted(
+        itertools.product(range(4), range(4), range(4), range(2)),
+        key=lambda t: -(2 * sum(min(u, 4 - u) for u in t[:3]) + t[3]),
+    )[:-1]
+    xs = [lax.rem(x + a, 4) * (2 * n_mp) for a in range(4)]
+    ys = [lax.rem(y_hi * 2 + y_lo + a, 4) for a in range(4)]
+    ys = [lax.div(y, 2) * (8 * n_mp) + lax.rem(y, 2) for y in ys]
+    zs = [lax.rem(z + a, 4) * 2 for a in range(4)]
+    cs = [lax.rem(core + a, 2) * n_mp for a in range(2)]
+    for a, b, c, e in moves:
+        copy = pltpu.make_async_remote_copy(
+            src_ref=mbuf.at[me], dst_ref=mbuf.at[me], send_sem=m_send, recv_sem=m_recv,
+            device_id=xs[a] + ys[b] + zs[c] + cs[e], device_id_type=pl.DeviceIdType.LOGICAL,
+        )
+        copy.start()
+    settle(mbuf.at[pl.ds(0, n_dp * n_mp - 1)], m_send, m_recv).wait_recv()
+    line = mbuf[0]
+    for d in range(1, n_dp * n_mp):
+        line = line + mbuf[d]
     mean_ref[...] = line * (1.0 / pool)
 
     settle(abuf.at[pl.ds(0, n_dp - 1)], a_send, a_recv).wait_send()
     settle(nbuf.at[pl.ds(0, n_mp - 1)], n_send, n_recv).wait_send()
     settle(bbuf.at[pl.ds(0, n_mp - 1)], b_send, b_recv).wait_send()
-    settle(m1.at[pl.ds(0, n_mp - 1)], s1, r1).wait_send()
-    settle(m2.at[pl.ds(0, n_dp - 1)], s2, r2).wait_send()
+    settle(mbuf.at[pl.ds(0, n_dp * n_mp - 1)], m_send, m_recv).wait_send()
 
 
 def body(n_dp, n_mp, hidden_states, factor_values, class_ids, centers):
@@ -212,25 +240,24 @@
     least, means = pl.pallas_call(
         functools.partial(kernel, n_dp, n_mp, rows_all * n_dp),
         out_shape=(
-            jax.ShapeDtypeStruct((1, rows), F32),
-            jax.ShapeDtypeStruct((1, 128), F32),
+            pltpu.VMEM((1, rows), F32),
+            pltpu.VMEM((1, 128), F32),
         ),
-        in_specs=[pl.BlockSpec(memory_space=pl.ANY)] * 3
-        + [pl.BlockSpec(memory_space=pltpu.SMEM)],
+        in_specs=[pl.BlockSpec(memory_space=pl.ANY)] * 4,
         out_specs=(pl.BlockSpec(memory_space=pltpu.VMEM),) * 2,
         scratch_shapes=[
             pltpu.VMEM((rows_all // 16, 16, width), BF16),
             pltpu.VMEM((k_loc, rows_all), BF16),
             pltpu.VMEM((k_loc, rows_all), jnp.int32),
+            pltpu.SMEM((STEPS,), jnp.int32),
             pltpu.VMEM((n_dp, 16, 128), BF16),
             pltpu.VMEM((n_mp, 1, 128), F32),
             pltpu.VMEM((n_mp, 8, rows), F32),
             pltpu.VMEM((n_mp, 8, rows), F32),
-            pltpu.VMEM((n_mp, 1, 128), F32),
-            pltpu.VMEM((n_dp, 1, 128), F32),
-            dma((3,)),
+            pltpu.VMEM((n_dp * n_mp, 1, 128), F32),
+            dma((4,)),
         ]
-        + [dma(())] * 10,
+        + [dma(())] * 8,
         compiler_params=pltpu.CompilerParams(collective_id=0, has_side_effects=True),
         name="badge",
     )(hidden_states.reshape(rows_all // 16, 16, width), factor_values.T, class_ids.T, centers)

time: 32.4 us -> 26.3 us (0.81)
  Pallas kernels: 29.3 us -> 24.5 us
  local copies, waits for them, and re-layouts: 2.39 us -> 1.09 us
    pallas_call x1, Pallas kernels: 29.3 us -> 24.5 us  [body(): pl.pallas_call(functools.partial(kernel, n_dp, n_mp, rows_all * n_dp), ou...]
    unnamed x1, local copies, waits for them, and re-layouts: 1.25 us -> 0.58 us
    squeeze x1, local copies, waits for them, and re-layouts: 1.14 us -> 0.51 us  [body(): return (least.reshape(rows), means[0, :STEPS])]
where the time goes in v2:
time: 26.3 us; the launch traced here: 26.2 us
  Pallas kernels  24.5 us (93%)
  local copies, waits for them, and re-layouts  1.09 us (4%)
  between operations  0.64 us (2%)
    pallas_call x1, Pallas kernels, body(): pl.pallas_call(functools.partial(kernel, n_dp, n_mp, rows_all * n_dp), ou...  24.5 us
    unnamed x1, local copies, waits for them, and re-layouts  0.58 us

profile of v2, /device:TPU:1, one launch (start us, length us, event | category | flops | bytes accessed | tf_op | source)
XLA Modules:
  0.0 26.2 jit_solution(7509144912287993250)
XLA Ops:
  0.6 24.5 %badge.1 = (f32[1,512]{1,0:T(1,128)S(1)}, f32[1,128]{1,0:T(1,128)S(1)}) custom-call(bf16[256,16,512]{2,1,0:T(8,128)(2,1)} %bitcast.7, bf16[16,4096]{1,0:T(8,128)(2,1)} %bitcast.9, s32[16,4096]{1,0:T(8,128)} %bitcast.8, s32[3]{0:T(128)} %c_hbm.1), custom_call_target="tpu_custom_call" | custom-call | tf_op jit(solution)/shard_map/badge/pallas_call | solution.py:240
  25.1 0.6 %copy.7 = f32[512]{0:T(512)} copy(f32[512]{0:T(512)S(1)} %bitcast.6) | data formatting | bytes 4096
  25.7 0.5 %slice_bitcast_fusion = f32[3]{0:T(128)} fusion(f32[1,128]{1,0:T(1,128)S(1)} %get-tuple-element.5), kind=kLoop, calls=%fused_computation | loop fusion | bytes 24 | tf_op jit(solution)/shard_map/squeeze | solution.py:264

commit v3 on v2

--- a/solution.py
+++ b/solution.py
@@ -224,12 +224,23 @@
     line = mbuf[0]
     for d in range(1, n_dp * n_mp):
         line = line + mbuf[d]
-    mean_ref[...] = line * (1.0 / pool)
+    mean_ref[...] = line[:, 0:STEPS] * (1.0 / pool)
 
     settle(abuf.at[pl.ds(0, n_dp - 1)], a_send, a_recv).wait_send()
     settle(nbuf.at[pl.ds(0, n_mp - 1)], n_send, n_recv).wait_send()
     settle(bbuf.at[pl.ds(0, n_mp - 1)], b_send, b_recv).wait_send()
     settle(mbuf.at[pl.ds(0, n_dp * n_mp - 1)], m_send, m_recv).wait_send()
+
+
+def put(least_ref, mean_ref, least_hbm, mean_hbm, sem):
+    copies = [
+        pltpu.make_async_copy(least_ref, least_hbm, sem.at[0]),
+        pltpu.make_async_copy(mean_ref, mean_hbm, sem.at[1]),
+    ]
+    for copy in copies:
+        copy.start()
+    for copy in copies:
+        copy.wait()
 
 
 def body(n_dp, n_mp, hidden_states, factor_values, class_ids, centers):
@@ -241,7 +252,7 @@
         functools.partial(kernel, n_dp, n_mp, rows_all * n_dp),
         out_shape=(
             pltpu.VMEM((1, rows), F32),
-            pltpu.VMEM((1, 128), F32),
+            pltpu.VMEM((1, STEPS), F32),
         ),
         in_specs=[pl.BlockSpec(memory_space=pl.ANY)] * 4,
         out_specs=(pl.BlockSpec(memory_space=pltpu.VMEM),) * 2,
@@ -261,7 +272,18 @@
         compiler_params=pltpu.CompilerParams(collective_id=0, has_side_effects=True),
         name="badge",
     )(hidden_states.reshape(rows_all // 16, 16, width), factor_values.T, class_ids.T, centers)
-    return least.reshape(rows), means[0, :STEPS]
+    least, means = pl.pallas_call(
+        put,
+        out_shape=(
+            jax.ShapeDtypeStruct((1, rows), F32),
+            jax.ShapeDtypeStruct((1, STEPS), F32),
+        ),
+        in_specs=[pl.BlockSpec(memory_space=pltpu.VMEM)] * 2,
+        out_specs=(pl.BlockSpec(memory_space=pl.ANY),) * 2,
+        scratch_shapes=[dma((2,))],
+        name="put",
+    )(*(pltpu.with_memory_space_constraint(a, pltpu.VMEM) for a in (least, means)))
+    return least.reshape(rows), means.reshape(STEPS)
 
 
 def solution(mesh):

time: 26.3 us -> 25.8 us (0.981)
  local copies, waits for them, and re-layouts: 1.09 us -> 0 us
  Pallas kernels: 24.5 us -> 25.1 us
    pallas_call x0 -> x1, Pallas kernels: none -> 0.6 us  [body(): pl.pallas_call(put, out_shape=(jax.ShapeDtypeStruct((1, rows), F32), jax....]
    unnamed x1 -> x0, local copies, waits for them, and re-layouts: 0.58 us -> none
    squeeze x1 -> x0, local copies, waits for them, and re-layouts: 0.51 us -> none  [body(): return (least.reshape(rows), means[0, :STEPS])]
where the time goes in v3:
time: 25.8 us; the launch traced here: 25.7 us
  Pallas kernels  25.1 us (97%)
  between operations  0.64 us (2%)
    pallas_call x1, Pallas kernels, body(): pl.pallas_call(functools.partial(kernel, n_dp, n_mp, rows_all * n_dp), ou...  24.5 us
    pallas_call x1, Pallas kernels, body(): pl.pallas_call(put, out_shape=(jax.ShapeDtypeStruct((1, rows), F32), jax....  0.6 us

profile of v3, /device:TPU:1, one launch (start us, length us, event | category | flops | bytes accessed | tf_op | source)
XLA Modules:
  0.0 25.7 jit_solution(2749638655754128082)
XLA Ops:
  0.6 24.5 %badge.1 = (f32[1,512]{1,0:T(1,128)S(1)}, f32[1,3]{1,0:T(1,128)S(1)}) custom-call(bf16[256,16,512]{2,1,0:T(8,128)(2,1)} %bitcast.5, bf16[16,4096]{1,0:T(8,128)(2,1)} %bitcast.7, s32[16,4096]{1,0:T(8,128)} %bitcast.6, s32[3]{0:T(128)} %c_hbm.1), custom_call_target="tpu_custom_call" | custom-call | tf_op jit(solution)/shard_map/badge/pallas_call | solution.py:251
  25.1 0.6 %put.1 = (f32[1,512]{1,0:T(1,128)}, f32[1,3]{1,0:T(1,128)}) custom-call(f32[1,512]{1,0:T(1,128)S(1)} %get-tuple-element.6.least_ref, f32[1,3]{1,0:T(1,128)S(1)} %get-tuple-element.7.mean_ref), custom_call_target="tpu_custom_call" | custom-call | tf_op jit(solution)/shard_map/put/pallas_call | solution.py:275
